TPU v7x, 32 devices: a 4x4x1 block of a 4x4x8 slice. The times are simulated.
32 devices in a mesh: part: 1 (over z), tp: 4 (over y), dp: 8 (over x, core).
Axes of the slice: x: 4, y: 4, z: 1, core: 2. Of those that a mesh axis runs over, the one named last changes fastest.
The devices are a block of a 4x4x8 slice.
Arguments:
- hidden: bfloat16 [128, 512, 768], P(('part', 'dp', 'tp'))
- ln_gain: float32 [768], replicated
- w_in: bfloat16 [768, 7040], P(None, ('dp', 'tp'))
- w_out: bfloat16 [3840, 768], P(('dp', 'tp'))
Outputs:
- output 1: bfloat16 [128, 512, 768], P(('part', 'dp', 'tp'))
- output 2: bfloat16 [128, 512, 64], P(('part', 'dp', 'tp'))
- output 3: bfloat16 [128, 512, 64], P(('part', 'dp', 'tp'))
All inputs are finite; a program needn't handle non-finite values.
Results may differ from a plain program's by a relative error of at most 0.00375414.
Values are sent between devices in bfloat16 or wider.
A program may use at most 768 MiB of HBM per device.

v0:
```python
import jax
import jax.numpy as jnp
from jax import lax
from jax.sharding import PartitionSpec as P

LN_EPS = 1e-6
ROPE_BASE = 10000.0
BLOCK_CAP = 512


def layer_norm(x_blk, ln_gain):
    x_wide = x_blk.astype(jnp.float32)
    centered = x_wide - jnp.mean(x_wide, axis=-1, keepdims=True)
    row_var = jnp.mean(centered * centered, axis=-1, keepdims=True)
    return (centered * lax.rsqrt(row_var + LN_EPS) * ln_gain).astype(jnp.bfloat16)


def rotary(values):
    seq_len = values.shape[1]
    head_dim = values.shape[-1]
    half_dim = head_dim // 2
    inv_freq = ROPE_BASE ** (-jnp.arange(half_dim, dtype=jnp.float32) * 2.0 / head_dim)
    angles = jnp.arange(seq_len, dtype=jnp.float32)[:, None] * inv_freq[None, :]
    tab_shape = (1, seq_len) + (1,) * (values.ndim - 3) + (half_dim,)
    cos_tab = jnp.cos(angles).reshape(tab_shape)
    sin_tab = jnp.sin(angles).reshape(tab_shape)
    first_half = values[..., :half_dim]
    second_half = values[..., half_dim:]
    return jnp.concatenate([first_half * cos_tab - second_half * sin_tab,
                            second_half * cos_tab + first_half * sin_tab], axis=-1)


def causal_mqa(q_rot, k_rot, v_all):
    n_batch, seq_len, n_heads, head_dim = q_rot.shape
    q_blk = min(seq_len, BLOCK_CAP)
    n_blk = seq_len // q_blk
    q_tiles = q_rot.reshape(n_batch, n_blk, q_blk, n_heads, head_dim)
    score_scale = head_dim ** -0.5
    key_pos = jnp.arange(seq_len)

    def one_block(blk_idx):
        q_tile = lax.dynamic_index_in_dim(q_tiles, blk_idx, axis=1, keepdims=False)
        scores = jnp.einsum('bqhe,bke->bqhk', q_tile, k_rot, preferred_element_type=jnp.float32) * score_scale
        q_pos = blk_idx * q_blk + jnp.arange(q_blk)
        allowed = key_pos[None, :] <= q_pos[:, None]
        scores = jnp.where(allowed[None, :, None, :], scores, -1e30)
        attn_prob = jax.nn.softmax(scores, axis=-1).astype(jnp.bfloat16)
        return jnp.einsum('bqhk,bke->bqhe', attn_prob, v_all, preferred_element_type=jnp.float32).astype(jnp.bfloat16)

    out_tiles = lax.map(one_block, jnp.arange(n_blk))
    return jnp.moveaxis(out_tiles, 0, 1).reshape(n_batch, seq_len, n_heads * head_dim)


def mix_rows(joint_rows, q_width, head_dim):
    n_batch, seq_len, joint_width = joint_rows.shape
    ff_width = (joint_width - q_width - 2 * head_dim) // 2
    gate_at = q_width + 2 * head_dim
    q_raw = joint_rows[..., :q_width].reshape(n_batch, seq_len, q_width // head_dim, head_dim)
    k_raw = joint_rows[..., q_width:q_width + head_dim]
    v_all = joint_rows[..., q_width + head_dim:gate_at]
    gate_proj = joint_rows[..., gate_at:gate_at + ff_width]
    up_proj = joint_rows[..., gate_at + ff_width:]
    q_rot = rotary(q_raw.astype(jnp.float32)).astype(jnp.bfloat16)
    k_rot = rotary(k_raw.astype(jnp.float32)).astype(jnp.bfloat16)
    attn_out = causal_mqa(q_rot, k_rot, v_all)
    mlp_out = (jax.nn.silu(gate_proj.astype(jnp.float32)) * up_proj.astype(jnp.float32)).astype(jnp.bfloat16)
    return jnp.concatenate([attn_out, mlp_out], axis=-1), k_rot, v_all


def solution(mesh):
    tok_spec = P(('part', 'dp', 'tp'))

    def per_device(x_blk, ln_gain, w_in_blk, w_out_blk):
        w_in = lax.all_gather(w_in_blk, ('dp', 'tp'), axis=1, tiled=True)
        w_out = lax.all_gather(w_out_blk, ('dp', 'tp'), axis=0, tiled=True)
        ff_width = 4 * x_blk.shape[-1]
        q_width = w_out.shape[0] - ff_width
        head_dim = (w_in.shape[1] - w_out.shape[0] - ff_width) // 2
        h_rows = layer_norm(x_blk, ln_gain)
        joint_rows = jnp.einsum('bsd,dc->bsc', h_rows, w_in, preferred_element_type=jnp.float32).astype(jnp.bfloat16)
        mixed_rows, k_rot, v_all = mix_rows(joint_rows, q_width, head_dim)
        proj_out = jnp.einsum('bsz,zd->bsd', mixed_rows, w_out, preferred_element_type=jnp.float32)
        y_blk = (x_blk.astype(jnp.float32) + proj_out).astype(jnp.bfloat16)
        return y_blk, k_rot, v_all

    return jax.shard_map(per_device, mesh=mesh,
                         in_specs=(tok_spec, P(), P(None, ('dp', 'tp')), P(('dp', 'tp'), None)),
                         out_specs=(tok_spec, tok_spec, tok_spec), check_vma=False)
```

profile of v0, /device:TPU:97, one launch (start us, length us, event | category | flops | bytes accessed | tf_op | source)
XLA Modules:
  0.0 230.0 jit_solution(7666339203130198751)
XLA Ops:
  7.2 0.1 all-gather.6.cloned.1.call-start
  7.2 0.7 all-gather.6.cloned.1.call-update
  8.0 0.1 all-gather.4.cloned.1.call-start
  8.0 0.7 all-gather.4.cloned.1.call-update
  8.8 0.8 iota_compare_fusion
  9.6 2.4 %convert_reduce_fusion = f32[4,512]{1,0:T(4,128)S(1)} fusion(bf16[4,512,768]{2,1,0:T(8,128)(2,1)} %param.4), kind=kLoop, calls=%fused_computation.23 | loop fusion | flops 3143680 | bytes 3153920 | tf_op jit(solution)/shard_map/reduce_sum | solution.py:13
  12.0 2.9 %fusion.19 = f32[4,512]{1,0:T(4,128)S(1)} fusion(bf16[4,512,768]{2,1,0:T(8,128)(2,1)} %param.4, f32[4,512]{1,0:T(4,128)S(1)} %broadcast_multiply_fusion), kind=kLoop, calls=%fused_computation.27 | loop fusion | flops 6289408 | bytes 3162112 | tf_op jit(solution)/shard_map/reduce_sum | solution.py:14
  14.9 0.3 fusion.40
  15.2 0.1 copy.36
  15.4 0.8 copy.37
  16.2 0.0 copy-start
  16.2 51.7 %all-gather.6.cloned.1.call-done = bf16[32,220,768]{2,1,0:T(8,128)(2,1)} async-done(((bf16[1,220,768]{2,1,0:T(8,128)(2,1)}), bf16[32,220,768]{2,1,0:T(8,128)(2,1)}) %all-gather.6.cloned.1.call-update) | async-done | bytes 10813456 | tf_op jit(solution)/shard_map/all_gather | solution.py:74
  67.9 13.8 %reshape.137 = bf16[7040,768,1]{1,0,2:T(8,128)(2,1)} reshape(bf16[32,220,768]{2,1,0:T(8,128)(2,1)} %all-gather.6.cloned.1.call-done) | data formatting | bytes 21626880
  81.7 0.0 copy-done
  81.7 31.2 %convolution_convert_fusion = bf16[4,512,7040]{2,1,0:T(8,128)(2,1)} fusion(bf16[7040,768,1]{1,0,2:T(8,128)(2,1)} %reshape.137, bf16[4,512,768]{2,1,0:T(8,128)(2,1)S(1)} %copy-done, f32[768]{0:T(1024)} %param.5, f32[4,512]{1,0:T(4,128)S(1)} %add_rsqrt_fusion, f32[4,512]{1,0:T(4,128)S(1)} %broadcast_multiply_fusion), kind=kOutput, calls=%fused_computation.16 | convolution fusion | flops 22168207360 | bytes 42814464 | tf_op jit(solution)/shard_map/bsd,dc->bsc/dot_general | solution.py:80
  112.9 2.6 %fusion.49 = (bf16[4,512,64]{2,1,0:T(8,128)(2,1)}, f32[4,512,64]{2,1,0:T(8,128)}) fusion(bf16[4,512,7040]{2,1,0:T(8,128)(2,1)} %convolution_convert_fusion), kind=kLoop, calls=%fused_computation.61 | loop fusion | flops 131072 | bytes 1310720 | tf_op jit(solution)/shard_map/slice | solution.py:60
  115.5 5.1 %slice_convert_fusion = f32[4,512,768]{2,1,0:T(8,128)} fusion(bf16[4,512,7040]{2,1,0:T(8,128)(2,1)} %convolution_convert_fusion), kind=kLoop, calls=%fused_computation.32 | loop fusion | flops 1572864 | bytes 9437184 | tf_op jit(solution)/shard_map/convert_element_type | solution.py:63
  120.6 6.6 %copy.35 = f32[4,512,768]{1,2,0:T(8,128)} copy(f32[4,512,768]{2,1,0:T(8,128)} %slice_convert_fusion) | data formatting | bytes 12582912 | tf_op jit(solution)/shard_map/convert_element_type | solution.py:63
  127.2 0.0 copy-start.1
  127.2 0.0 copy-start.2
  127.2 5.7 %subtract_convert_fusion = (bf16[4,512,12,32]{1,3,2,0:T(8,128)(2,1)}, bf16[4,512,12,32]{1,3,2,0:T(8,128)(2,1)}) fusion(f32[4,512,12,64]{1,3,2,0:T(8,128)} %bitcast.29, f32[512,32]{0,1:T(8,128)S(1)} %get-tuple-element.40, f32[512,32]{0,1:T(8,128)S(1)} %get-tuple-element.39), kind=kLoop, calls=%fused_computation.35 | loop fusion | flops 6291456 | bytes 9568256 | tf_op jit(solution)/shard_map/convert.3
  132.9 0.0 copy-done.1
  132.9 0.0 copy-done.2
  132.9 0.4 subtract_convert_fusion.1
  133.4 1.1 pad_maximum_fusion.7
  134.5 1.9 copy.42
  136.4 24.9 %fusion.50 = (f32[4,512,12]{1,2,0:T(8,128)S(1)}, f32[4,512,12,512]{1,3,2,0:T(8,128)}) fusion(pred[512,512]{0,1:T(8,128)(4,1)} %iota_compare_fusion, bf16[4,512,12,32]{1,3,2,0:T(8,128)(2,1)} %get-tuple-element.36, bf16[4,512,12,32]{1,3,2,0:T(8,128)(2,1)} %get-tuple-element.35, bf16[4,512,64]{2,1,0:T(8,128)(2,1)} %pad_maximum_fusion.7), kind=kOutput, calls=%fused_computation.62 | convolution fusion | flops 1667236352 | bytes 54099968 | tf_op jit(solution)/shard_map/while/body/eval_jaxpr/sub | solution.py:47
  161.3 20.2 %fusion.28 = bf16[4,512,12,64]{1,3,2,0:T(8,128)(2,1)} fusion(f32[4,512,12,512]{1,3,2,0:T(8,128)} %get-tuple-element.42, f32[4,512,12]{1,2,0:T(8,128)S(1)} %get-tuple-element.41, bf16[4,512,7040]{2,1,0:T(8,128)(2,1)} %convolution_convert_fusion), kind=kOutput, calls=%fused_computation.39 | convolution fusion | flops 1637351424 | bytes 54099968 | tf_op jit(solution)/shard_map/while/body/eval_jaxpr/bqhk,bke->bqhe/dot_general | solution.py:48
  181.5 4.7 %copy.41 = bf16[4,512,768]{2,1,0:T(8,128)(2,1)} copy(bf16[4,512,768]{1,2,0:T(8,128)(2,1)} %bitcast.30) | data formatting | bytes 6291456 | tf_op jit(solution)/shard_map/reshape;transpose | solution.py:51
  186.2 1.9 copy.43
  188.1 16.4 %fusion.8 = bf16[4,512,3072]{2,1,0:T(8,128)(2,1)} fusion(bf16[4,512,7040]{2,1,0:T(8,128)(2,1)} %convolution_convert_fusion), kind=kLoop, calls=%fused_computation.13 | loop fusion | flops 50331648 | bytes 37748736 | tf_op jit(solution)/shard_map/convert_element_type | solution.py:66
  204.5 0.0 all-gather.4.cloned.1.call-done
  204.5 18.6 %fusion.22 = bf16[4,512,768]{2,1,0:T(8,128)(2,1)} fusion(bf16[4,512,768]{2,1,0:T(8,128)(2,1)S(1)} %copy-done, bf16[3840,768]{1,0:T(8,128)(2,1)} %all-gather.4.cloned.1.call-done, bf16[4,512,3072]{2,1,0:T(8,128)(2,1)} %fusion.8, bf16[4,512,768]{2,1,0:T(8,128)(2,1)} %copy.41), kind=kOutput, calls=%fused_computation.30 | convolution fusion | flops 12115771392 | bytes 27918336 | tf_op jit(solution)/shard_map/bsz,zd->bsd/dot_general | solution.py:82
  (3 shorter events, 0.0 us)
Async XLA Ops:
  7.2 60.7 %all-gather.6.cloned.1.call-start = ((), (), s32[]{:S(2)}) async-start(), calls=%async_computation.1 | async-start | bytes 11354112 | tf_op jit(solution)/shard_map/all_gather | solution.py:74
  8.0 196.6 %all-gather.4.cloned.1.call-start = ((), (), s32[]{:S(2)}) async-start(), calls=%async_computation | async-start | bytes 6082560 | tf_op jit(solution)/shard_map/all_gather | solution.py:75
  16.2 65.5 %copy-start = (bf16[4,512,768]{2,1,0:T(8,128)(2,1)S(1)}, bf16[4,512,768]{2,1,0:T(8,128)(2,1)}, u32[]{:S(2)}) copy-start(bf16[4,512,768]{2,1,0:T(8,128)(2,1)} %param.4) | copy-start | bytes 9437188
  127.2 5.7 %copy-start.1 = (f32[4,512,64]{2,1,0:T(8,128)S(1)}, f32[4,512,64]{2,1,0:T(8,128)}, u32[]{:S(2)}) copy-start(f32[4,512,64]{2,1,0:T(8,128)} %get-tuple-element.34) | copy-start | bytes 1572868
  127.2 5.7 %copy-start.2 = (f32[512,32]{1,0:T(8,128)S(1)}, f32[512,32]{1,0:T(8,128)}, u32[]{:S(2)}) copy-start(f32[512,32]{1,0:T(8,128)} %copy.37) | copy-start | bytes 196612
Sparse Core Ops, SparseCore 0:
  10.1 57.7 all-gather.5
  70.1 42.6 all-gather.3
where the time goes:
time: 231 us; the launch traced here: 230 us
  matrix products  94.9 us (41%)
  waiting for transfers between devices  53.1 us (23%)
  other arithmetic  37.8 us (16%)
  local copies, waits for them, and re-layouts  29.9 us (13%)
  between operations  14.1 us (6%)
    all_gather x1, waiting for transfers between devices, per_device(): w_in = lax.all_gather(w_in_blk, ('dp', 'tp'), axis=1, tiled=True)  51.7 us
    dot_general x1, matrix products, per_device(): jnp.einsum('bsd,dc->bsc', h_rows, w_in, preferred_element_type=jnp.float32)  31.2 us
    sub x1, matrix products, one_block(): attn_prob = jax.nn.softmax(scores, axis=-1).astype(jnp.bfloat16)  24.9 us
    dot_general x1, matrix products, one_block(): jnp.einsum('bqhk,bke->bqhe', attn_prob, v_all, preferred_element_type=jnp...  20.2 us
    dot_general x1, matrix products, per_device(): jnp.einsum('bsz,zd->bsd', mixed_rows, w_out, preferred_element_type=jnp.f...  18.6 us
    unnamed x9, local copies, waits for them, and re-layouts  17.6 us
    convert_element_type x1, other arithmetic, mix_rows(): (jax.nn.silu(gate_proj.astype(jnp.float32)) * up_proj.astype(jnp.float32)...  16.4 us
    convert_element_type x1, local copies, waits for them, and re-layouts, mix_rows(): q_rot = rotary(q_raw.astype(jnp.float32)).astype(jnp.bfloat16)  6.58 us
  transfers between devices with their start and end apart: 2, of which 1 were waited for; matrix products, arithmetic and copies ran while one was open for 63% of the time, Pallas kernels for 0%

commit v1 on v0

v1 whole, which is shorter than its diff:
```python
import functools

import jax
import jax.numpy as jnp
import numpy as np
from jax import lax
from jax.experimental import pallas as pl
from jax.experimental.pallas import tpu as pltpu
from jax.sharding import PartitionSpec as P

LN_EPS = 1e-6
ROPE_BASE = 10000.0
MESH = pl.DeviceIdType.MESH
F32 = jnp.float32
BF16 = jnp.bfloat16


def nt_dot(lhs, rhs):
    return lax.dot_general(lhs, rhs, (((1,), (1,)), ((), ())), preferred_element_type=F32)


class Ring:
    def __init__(self, n, pos, right, left, block, send, recv):
        self.n, self.pos, self.right, self.left = n, pos, right, left
        self.block, self.send, self.recv = block, send, recv
        self.routes = ((0, 0, True), (0, 1, True), (1, 0, True), (0, 1, False), (0, 0, False), (1, 1, False))

    def _copy(self, k, hops):
        back, half, to_right = self.routes[k]
        step = (back + hops) if to_right else self.n - (back + hops)
        z = lax.rem(self.pos - step + 2 * self.n, self.n)
        ref = self.block(z, half)
        return pltpu.make_async_remote_copy(
            src_ref=ref, dst_ref=ref, send_sem=self.send(k), recv_sem=self.recv(k),
            device_id=self.right if to_right else self.left, device_id_type=MESH)

    def start(self):
        for k in (0, 3, 1, 4):
            self._copy(k, 0).start()

    def forward(self):
        self._copy(0, 1).wait_recv()
        self._copy(2, 0).start()
        self._copy(3, 1).wait_recv()
        self._copy(5, 0).start()

    def finish(self):
        for k in (1, 4, 2, 5):
            self._copy(k, 1).wait_recv()

    def drain(self):
        for k in range(6):
            self._copy(k, 0).wait_send()


def layer_kernel(n, x_hbm, gain_ref, wi_hbm, wo_hbm, cos_ref, sin_ref, y_hbm, kc_ref, vc_ref,
                 x_v, h_v, mixed, gi, go, wq, wg, wu, wo, qkv, kt,
                 x_sem, own_sem, y_sem, send_sem, recv_sem, psend_sem, precv_sem):
    n_req, seq, d = x_v.shape
    in_rows, half = gi.shape[2], gi.shape[3]
    out_rows = go.shape[2]
    n_dev = gi.shape[1]
    head = kc_ref.shape[1]
    q_width = wq.shape[0] - 2 * head
    ff = wo.shape[0] - q_width
    chunk = wg.shape[0]

    dp, tp = lax.axis_index("dp"), lax.axis_index("tp")
    core, x, y = lax.rem(dp, 2), dp // 2, tp
    a = (1 - core) * x + core * y
    b = (1 - core) * y + core * x

    def place(za, zb, c):
        zx = (1 - c) * za + c * zb
        zy = (1 - c) * zb + c * za
        return zx * 2 + c, zy

    def device(za, zb):
        zdp, ztp = place(lax.rem(za + n, n), lax.rem(zb + n, n), core)
        return {"dp": zdp, "tp": ztp}

    def shard(za, zb, c):
        zdp, ztp = place(za, zb, c)
        return zdp * n + ztp

    partner = {"dp": x * 2 + 1 - core, "tp": tp}
    bufs = (gi, go)
    me = dp * n + tp

    own = []
    for h in range(2):
        own.append(pltpu.make_async_copy(wi_hbm.at[:, pl.ds(h * half, half)], gi.at[h, me], own_sem.at[0, h]))
    for h in range(2):
        own.append(pltpu.make_async_copy(wo_hbm.at[:, pl.ds(h * half, half)], go.at[h, me], own_sem.at[1, h]))
    for copy in own:
        copy.start()
    x_in = [pltpu.make_async_copy(x_hbm.at[r], x_v.at[r], x_sem.at[r]) for r in range(n_req)]
    for copy in x_in:
        copy.start()

    barrier = pltpu.get_barrier_semaphore()
    for dev in (device(a + 1, b), device(a - 1, b), device(a, b + 1), device(a, b - 1), partner):
        pl.semaphore_signal(barrier, inc=1, device_id=dev, device_id_type=MESH)
    pl.semaphore_wait(barrier, 5)
    for copy in own:
        copy.wait()

    def first_ring(rnd):
        return Ring(n, a, device(a + 1, b), device(a - 1, b),
                    lambda z, h: bufs[rnd].at[h, shard(z, b, core)],
                    lambda k: send_sem.at[rnd, 0, k], lambda k: recv_sem.at[rnd, 0, k])

    def second_ring(rnd, s):
        return Ring(n, b, device(a, b + 1), device(a, b - 1),
                    lambda z, h: bufs[rnd].at[h, shard(s, z, core)],
                    lambda k: send_sem.at[rnd, 1 + s, k], lambda k: recv_sem.at[rnd, 1 + s, k])

    def pair_copy(rnd, s, k, mine):
        if mine:
            idx = shard(s, lax.rem(b + k, n), core)
        else:
            idx = shard(s, lax.rem(a + k, n), 1 - core)
        ref = bufs[rnd].at[:, idx]
        return pltpu.make_async_remote_copy(
            src_ref=ref, dst_ref=ref, send_sem=psend_sem.at[rnd, s, k], recv_sem=precv_sem.at[rnd, s, k],
            device_id=partner, device_id_type=MESH)

    firsts = [first_ring(r) for r in range(2)]
    seconds = [[second_ring(r, s) for s in range(n)] for r in range(2)]

    def finish_second(rnd, s):
        seconds[rnd][s].finish()
        for k in range(1, n):
            pair_copy(rnd, s, k, True).start()

    def start_second(rnd, s):
        seconds[rnd][s].start()
        pair_copy(rnd, s, 0, True).start()

    def from_partner(rnd, s):
        for k in range(n):
            pair_copy(rnd, s, k, False).wait_recv()

    firsts[0].start()

    gain = gain_ref[...]
    ln_rows = 128

    def norm_rows(r):
        def body(i, carry):
            rows = pl.ds(pl.multiple_of(i * ln_rows, ln_rows), ln_rows)
            xw = x_v[r, rows, :].astype(F32)
            cen = xw - jnp.mean(xw, axis=-1, keepdims=True)
            var = jnp.mean(cen * cen, axis=-1, keepdims=True)
            h_v[r, rows, :] = (cen * lax.rsqrt(var + LN_EPS) * gain).astype(BF16)
            return carry
        lax.fori_loop(0, seq // ln_rows, body, 0)

    x_in[0].wait()
    norm_rows(0)
    firsts[0].forward()
    x_in[1].wait()
    norm_rows(1)
    firsts[0].finish()
    start_second(0, 0)
    for r in range(2, n_req):
        x_in[r].wait()
        norm_rows(r)
    seconds[0][0].forward()
    for s in range(1, n):
        start_second(0, s)
    finish_second(0, 0)
    from_partner(0, 0)

    def assemble(dst, src, rows_per, start, count):
        row = start
        while row < start + count:
            blk, r0 = row // rows_per, row % rows_per
            take = min(rows_per - r0, start + count - row)
            for h in range(2):
                dst[row - start:row - start + take, h * half:(h + 1) * half] = src[h, blk, r0:r0 + take, :]
            row += take

    assemble(wq, gi, in_rows, 0, q_width + 2 * head)

    hd2 = head // 2
    scale = head ** -0.5
    qb = seq // 2
    key_idx = lax.broadcasted_iota(jnp.int32, (qb, qb), 0)
    qry_idx = lax.broadcasted_iota(jnp.int32, (qb, qb), 1)

    def rotate(u):
        cos, sin = cos_ref[...], sin_ref[...]
        first, second = u[:hd2].astype(F32), u[hd2:].astype(F32)
        return jnp.concatenate([first * cos - second * sin, second * cos + first * sin], axis=0).astype(BF16)

    def softmax_pv(blocks, vt):
        top = functools.reduce(jnp.maximum, [jnp.max(s, axis=0, keepdims=True) for s in blocks])
        probs = [jnp.exp((s - top) * scale) for s in blocks]
        total = functools.reduce(jnp.add, [jnp.sum(p, axis=0, keepdims=True) for p in probs])
        wide = probs[0] if len(probs) == 1 else jnp.concatenate(probs, axis=0)
        out = jnp.dot(vt, wide.astype(BF16), preferred_element_type=F32)
        return out / total

    def attend(r):
        h_r = h_v[r]
        qkv[...] = nt_dot(wq[...], h_r).astype(BF16)
        k_rot = rotate(qkv[q_width:q_width + head, :])
        kc_ref[r] = k_rot
        vc_ref[r] = qkv[q_width + head:, :]
        kt[...] = k_rot.astype(F32).T.astype(BF16)

        def one_head(row):
            q_rot = rotate(qkv[pl.ds(row, head), :])
            vt = vc_ref[r]
            s_a = jnp.dot(kt[:qb], q_rot[:, :qb], preferred_element_type=F32)
            s_b = jnp.dot(kt[:qb], q_rot[:, qb:], preferred_element_type=F32)
            s_c = jnp.dot(kt[qb:], q_rot[:, qb:], preferred_element_type=F32)
            allowed = key_idx <= qry_idx
            o_a = softmax_pv([jnp.where(allowed, s_a, -1e30)], vt[:, :qb])
            o_b = softmax_pv([s_b, jnp.where(allowed, s_c, -1e30)], vt)
            return jnp.concatenate([o_a, o_b], axis=1)

        def body(i, carry):
            row = pl.multiple_of(i * 2 * head, 2 * head)
            pair = jnp.concatenate([one_head(row), one_head(row + head)], axis=0)
            mixed[r, :, pl.ds(row, 2 * head)] = pair.T.astype(BF16)
            return carry

        lax.fori_loop(0, q_width // (2 * head), body, 0)

    attend(0)
    seconds[0][1].forward()
    firsts[1].start()
    attend(1)
    finish_second(0, 1)
    seconds[0][2].forward()
    seconds[0][3].forward()
    attend(2)
    finish_second(0, 2)
    finish_second(0, 3)
    firsts[1].forward()
    attend(3)
    firsts[1].finish()
    for s in range(n):
        start_second(1, s)
    for s in range(1, n):
        from_partner(0, s)

    gate_at = q_width + 2 * head
    tok = 256
    tiles = seq // tok

    def mlp_chunk(c):
        assemble(wg, gi, in_rows, gate_at + c * chunk, chunk)
        assemble(wu, gi, in_rows, gate_at + ff + c * chunk, chunk)

        def body(i, carry):
            r = i // tiles
            rows = pl.ds(pl.multiple_of((i - r * tiles) * tok, tok), tok)
            h_t = h_v[r, rows, :]
            g = nt_dot(h_t, wg[...]).astype(BF16).astype(F32)
            u = nt_dot(h_t, wu[...]).astype(BF16).astype(F32)
            act = 0.5 * g * (1.0 + jnp.tanh(0.5 * g))
            mixed[r, rows, q_width + c * chunk:q_width + (c + 1) * chunk] = (act * u).astype(BF16)
            return carry
        lax.fori_loop(0, n_req * tiles, body, 0)

    for c in range(ff // chunk):
        mlp_chunk(c)
        if c < n:
            seconds[1][c].forward()
        if 1 <= c <= n:
            finish_second(1, c - 1)
    for s in range(n):
        from_partner(1, s)

    assemble(wo, go, out_rows, 0, q_width + ff)

    def y_copy(r, t):
        rows = pl.ds(pl.multiple_of(t * tok, tok), tok)
        return pltpu.make_async_copy(x_v.at[r, rows], y_hbm.at[r, rows], y_sem.at[r, t])

    def out_body(i, carry):
        r = i // tiles
        t = i - r * tiles
        rows = pl.ds(pl.multiple_of(t * tok, tok), tok)
        acc = jnp.dot(mixed[r, rows, :], wo[...], preferred_element_type=F32)
        x_v[r, rows, :] = (x_v[r, rows, :].astype(F32) + acc).astype(BF16)
        y_copy(r, t).start()
        return carry
    lax.fori_loop(0, n_req * tiles, out_body, 0)

    for r in range(n_req):
        for t in range(tiles):
            y_copy(r, t).wait()
    for rnd in range(2):
        firsts[rnd].drain()
        for s in range(n):
            seconds[rnd][s].drain()
            for k in range(n):
                pair_copy(rnd, s, k, True).wait_send()


def rope_tables(seq, head):
    inv_freq = (np.float32(ROPE_BASE) ** (-np.arange(head // 2, dtype=np.float32) * np.float32(2.0) / np.float32(head)))
    angles = inv_freq.astype(np.float32)[:, None] * np.arange(seq, dtype=np.float32)[None, :]
    return np.cos(angles).astype(np.float32), np.sin(angles).astype(np.float32)


def solution(mesh):
    tok_spec = P(('part', 'dp', 'tp'))
    n = mesh.shape['tp']
    n_dev = n * mesh.shape['dp']

    def per_device(x_blk, ln_gain, w_in_blk, w_out_blk):
        n_req, seq, d = x_blk.shape
        in_rows, out_rows = w_in_blk.shape[1], w_out_blk.shape[0]
        ff = 4 * d
        q_width = out_rows * n_dev - ff
        head = (in_rows * n_dev - q_width - 2 * ff) // 2
        chunk = min(512, ff)
        cos, sin = rope_tables(seq, head)
        vmem = pl.BlockSpec(memory_space=pltpu.VMEM)
        anyw = pl.BlockSpec(memory_space=pl.ANY)
        tiles = seq // 256
        y, kc, vc = pl.pallas_call(
            functools.partial(layer_kernel, n),
            out_shape=(jax.ShapeDtypeStruct(x_blk.shape, BF16),
                       jax.ShapeDtypeStruct((n_req, head, seq), BF16),
                       jax.ShapeDtypeStruct((n_req, head, seq), BF16)),
            in_specs=[anyw, vmem, anyw, anyw, vmem, vmem],
            out_specs=(anyw, vmem, vmem),
            scratch_shapes=[
                pltpu.VMEM((n_req, seq, d), BF16),
                pltpu.VMEM((n_req, seq, d), BF16),
                pltpu.VMEM((n_req, seq, q_width + ff), BF16),
                pltpu.VMEM((2, n_dev, in_rows, d // 2), BF16),
                pltpu.VMEM((2, n_dev, out_rows, d // 2), BF16),
                pltpu.VMEM((q_width + 2 * head, d), BF16),
                pltpu.VMEM((chunk, d), BF16),
                pltpu.VMEM((chunk, d), BF16),
                pltpu.VMEM((q_width + ff, d), BF16),
                pltpu.VMEM((q_width + 2 * head, seq), BF16),
                pltpu.VMEM((seq, head), BF16),
                pltpu.SemaphoreType.DMA((n_req,)),
                pltpu.SemaphoreType.DMA((2, 2)),
                pltpu.SemaphoreType.DMA((n_req, tiles)),
                pltpu.SemaphoreType.DMA((2, 1 + n, 6)),
                pltpu.SemaphoreType.DMA((2, 1 + n, 6)),
                pltpu.SemaphoreType.DMA((2, n, n)),
                pltpu.SemaphoreType.DMA((2, n, n)),
            ],
            compiler_params=pltpu.CompilerParams(
                collective_id=0, has_side_effects=True, vmem_limit_bytes=63 * 1024 * 1024),
        )(x_blk, ln_gain.reshape(1, d), w_in_blk.T, w_out_blk, cos, sin)
        return y, kc.swapaxes(1, 2), vc.swapaxes(1, 2)

    return jax.shard_map(per_device, mesh=mesh,
                         in_specs=(tok_spec, P(), P(None, ('dp', 'tp')), P(('dp', 'tp'), None)),
                         out_specs=(tok_spec, tok_spec, tok_spec), check_vma=False)
```

time: 231 us -> 115 us (0.50)
  Pallas kernels: 0 us -> 107 us
  matrix products: 94.9 us -> 0 us
  waiting for transfers between devices: 53.1 us -> 0 us
  other arithmetic: 37.8 us -> 0 us
  local copies, waits for them, and re-layouts: 29.9 us -> 6.49 us
  between operations: 14.1 us -> 0.66 us
    pallas_call x0 -> x1, Pallas kernels: none -> 107 us  [per_device(): pl.pallas_call(functools.partial(layer_kernel, n), out_shape=(jax.ShapeDt...]
    dot_general x3 -> x0, matrix products: 70 us -> none  [the longest x1 31.2 us: per_device(): jnp.einsum('bsd,dc->bsc', h_rows, w_in, preferred_element_type=jnp.float32)]
    all_gather x2 -> x0, waiting for transfers between devices: 51.7 us -> none  [the longest x1 51.7 us: per_device(): w_in = lax.all_gather(w_in_blk, ('dp', 'tp'), axis=1, tiled=True)]
    sub x1 -> x0, matrix products: 24.9 us -> none  [one_block(): attn_prob = jax.nn.softmax(scores, axis=-1).astype(jnp.bfloat16)]
    convert_element_type x2 -> x0, other arithmetic: 21.5 us -> none  [the longest x1 16.4 us: mix_rows(): (jax.nn.silu(gate_proj.astype(jnp.float32)) * up_proj.astype(jnp.float32)...]
    unnamed x9 -> x7, local copies, waits for them, and re-layouts: 17.6 us -> 5.22 us
    convert_element_type x1 -> x0, local copies, waits for them, and re-layouts: 6.58 us -> none  [mix_rows(): q_rot = rotary(q_raw.astype(jnp.float32)).astype(jnp.bfloat16)]
    another operation x2 -> x0, other arithmetic: 6.17 us -> none
  transfers between devices with their start and end apart: 2 -> 0, of which waited for: 1 -> 0; matrix products, arithmetic and copies ran while one was open for 63% -> 0% of each run, Pallas kernels for 0% -> 0%
where the time goes in v1:
time: 115 us
  Pallas kernels  107 us (93%)
  local copies, waits for them, and re-layouts  6.49 us (6%)
    pallas_call x1, Pallas kernels, per_device(): pl.pallas_call(functools.partial(layer_kernel, n), out_shape=(jax.ShapeDt...  107 us
    unnamed x7, local copies, waits for them, and re-layouts  5.22 us

profile of v1, /device:TPU:97, one launch (start us, length us, event | category | flops | bytes accessed | tf_op | source)
XLA Modules:
  0.0 114.6 jit_solution(637260683158214602)
XLA Ops:
  0.6 1.3 %reshape.9.gain_ref = f32[1,768]{1,0:T(1,128)} reshape(f32[768]{0:T(1024)} %param.7) | data formatting | bytes 6144 | tf_op jit(solution)/shard_map/reshape | solution.py:356
  1.9 107.5 %shard_map.85 = (bf16[4,512,768]{2,1,0:T(8,128)(2,1)}, bf16[4,64,512]{2,1,0:T(8,128)(2,1)}, bf16[4,64,512]{2,1,0:T(8,128)(2,1)}) custom-call(bf16[4,512,768]{2,1,0:T(8,128)(2,1)} %x_hbm.1, f32[1,768]{1,0:T(1,128)} %reshape.9.gain_ref, bf16[220,768]{1,0:T(8,128)(2,1)} %bitcast.3, bf16[120,768]{1,0:T(8,128)(2,1)} %wo_hbm.1, f32[32,512]{1,0:T(8,128)} %constant.4.clone.cos_ref, ...), custom_call_target="tpu_custom_call" | custom-call | tf_op jit(solution)/shard_map/pallas_call | solution.py:327
  109.4 0.0 copy-start.1
  109.4 0.0 copy-start
  109.4 3.8 %copy.12 = bf16[4,512,768]{2,1,0:T(8,128)(2,1)} copy(bf16[4,512,768]{2,1,0:T(8,128)(2,1)} %get-tuple-element.12) | data formatting | bytes 6291456
  113.2 0.0 copy-done.1
  113.2 0.7 copy.13
  113.9 0.0 copy-done
  113.9 0.7 copy.14
Async XLA Ops:
  109.4 3.8 %copy-start.1 = (bf16[4,64,512]{2,1,0:T(8,128)(2,1)S(1)}, bf16[4,64,512]{2,1,0:T(8,128)(2,1)}, u32[]{:S(2)}) copy-start(bf16[4,64,512]{2,1,0:T(8,128)(2,1)} %get-tuple-element.7) | copy-start | bytes 786436
  109.4 4.5 %copy-start = (bf16[4,64,512]{2,1,0:T(8,128)(2,1)S(1)}, bf16[4,64,512]{2,1,0:T(8,128)(2,1)}, u32[]{:S(2)}) copy-start(bf16[4,64,512]{2,1,0:T(8,128)(2,1)} %get-tuple-element.8) | copy-start | bytes 786436

commit v2 on v1

--- a/solution.py
+++ b/solution.py
@@ -54,7 +54,7 @@
 
 
 def layer_kernel(n, x_hbm, gain_ref, wi_hbm, wo_hbm, cos_ref, sin_ref, y_hbm, kc_ref, vc_ref,
-                 x_v, h_v, mixed, gi, go, wq, wg, wu, wo, qkv, kt,
+                 x_v, h_v, mixed, gi, go, wq, wg, wu, wo, qkv, kt, s_a, s_b,
                  x_sem, own_sem, y_sem, send_sem, recv_sem, psend_sem, precv_sem):
     n_req, seq, d = x_v.shape
     in_rows, half = gi.shape[2], gi.shape[3]
@@ -184,47 +184,64 @@
     assemble(wq, gi, in_rows, 0, q_width + 2 * head)
 
     hd2 = head // 2
-    scale = head ** -0.5
-    qb = seq // 2
-    key_idx = lax.broadcasted_iota(jnp.int32, (qb, qb), 0)
-    qry_idx = lax.broadcasted_iota(jnp.int32, (qb, qb), 1)
+    scale = float(head ** -0.5 * np.log2(np.e))
+    blk = 128
+    n_blk = seq // blk
+    key_idx = lax.broadcasted_iota(jnp.int32, (blk, blk), 0)
+    qry_idx = lax.broadcasted_iota(jnp.int32, (blk, blk), 1)
 
     def rotate(u):
         cos, sin = cos_ref[...], sin_ref[...]
         first, second = u[:hd2].astype(F32), u[hd2:].astype(F32)
         return jnp.concatenate([first * cos - second * sin, second * cos + first * sin], axis=0).astype(BF16)
 
-    def softmax_pv(blocks, vt):
-        top = functools.reduce(jnp.maximum, [jnp.max(s, axis=0, keepdims=True) for s in blocks])
-        probs = [jnp.exp((s - top) * scale) for s in blocks]
-        total = functools.reduce(jnp.add, [jnp.sum(p, axis=0, keepdims=True) for p in probs])
-        wide = probs[0] if len(probs) == 1 else jnp.concatenate(probs, axis=0)
-        out = jnp.dot(vt, wide.astype(BF16), preferred_element_type=F32)
-        return out / total
+    def scores(row, dst):
+        q_rot = rotate(qkv[pl.ds(row, head), :])
+        for t in range(0, seq, 2 * blk):
+            stop = t + 2 * blk
+            dst[:stop, t:stop] = jnp.dot(kt[:stop], q_rot[:, t:stop], preferred_element_type=F32)
+
+    def softmax_pv(src, r):
+        outs = []
+        for t in range(0, n_blk, 2):
+            cols, inv = [], []
+            for b_q in (t, t + 1):
+                lanes = slice(b_q * blk, (b_q + 1) * blk)
+                diag = jnp.where(key_idx <= qry_idx, src[lanes, lanes], -1e30)
+                top = jnp.max(diag, axis=0, keepdims=True)
+                if b_q:
+                    top = jnp.maximum(top, jnp.max(src[:b_q * blk, lanes], axis=0, keepdims=True))
+                p_diag = jnp.exp2((diag - top) * scale)
+                total = jnp.sum(p_diag, axis=0, keepdims=True)
+                parts = [p_diag.astype(BF16)]
+                if b_q:
+                    p_full = jnp.exp2((src[:b_q * blk, lanes] - top) * scale)
+                    total = total + jnp.sum(p_full, axis=0, keepdims=True)
+                    parts.insert(0, p_full.astype(BF16))
+                if b_q == t:
+                    parts.append(jnp.zeros((blk, blk), BF16))
+                cols.append(parts[0] if len(parts) == 1 else jnp.concatenate(parts, axis=0))
+                inv.append(1.0 / total)
+            probs = jnp.concatenate(cols, axis=1)
+            out = jnp.dot(vc_ref[r, :, :probs.shape[0]], probs, preferred_element_type=F32)
+            outs.append(out * jnp.concatenate(inv, axis=1))
+        return jnp.concatenate(outs, axis=1)
 
     def attend(r):
-        h_r = h_v[r]
-        qkv[...] = nt_dot(wq[...], h_r).astype(BF16)
+        qkv[...] = nt_dot(wq[...], h_v[r]).astype(BF16)
         k_rot = rotate(qkv[q_width:q_width + head, :])
         kc_ref[r] = k_rot
         vc_ref[r] = qkv[q_width + head:, :]
         kt[...] = k_rot.astype(F32).T.astype(BF16)
-
-        def one_head(row):
-            q_rot = rotate(qkv[pl.ds(row, head), :])
-            vt = vc_ref[r]
-            s_a = jnp.dot(kt[:qb], q_rot[:, :qb], preferred_element_type=F32)
-            s_b = jnp.dot(kt[:qb], q_rot[:, qb:], preferred_element_type=F32)
-            s_c = jnp.dot(kt[qb:], q_rot[:, qb:], preferred_element_type=F32)
-            allowed = key_idx <= qry_idx
-            o_a = softmax_pv([jnp.where(allowed, s_a, -1e30)], vt[:, :qb])
-            o_b = softmax_pv([s_b, jnp.where(allowed, s_c, -1e30)], vt)
-            return jnp.concatenate([o_a, o_b], axis=1)
+        scores(0, s_a)
 
         def body(i, carry):
             row = pl.multiple_of(i * 2 * head, 2 * head)
-            pair = jnp.concatenate([one_head(row), one_head(row + head)], axis=0)
-            mixed[r, :, pl.ds(row, 2 * head)] = pair.T.astype(BF16)
+            scores(row + head, s_b)
+            out_a = softmax_pv(s_a, r)
+            scores(jnp.minimum(row + 2 * head, q_width - head), s_a)
+            out_b = softmax_pv(s_b, r)
+            mixed[r, :, pl.ds(row, 2 * head)] = jnp.concatenate([out_a, out_b], axis=0).T.astype(BF16)
             return carry
 
         lax.fori_loop(0, q_width // (2 * head), body, 0)
@@ -248,7 +265,7 @@
         from_partner(0, s)
 
     gate_at = q_width + 2 * head
-    tok = 256
+    tok = 512
     tiles = seq // tok
 
     def mlp_chunk(c):
@@ -323,7 +340,7 @@
         cos, sin = rope_tables(seq, head)
         vmem = pl.BlockSpec(memory_space=pltpu.VMEM)
         anyw = pl.BlockSpec(memory_space=pl.ANY)
-        tiles = seq // 256
+        tiles = seq // 512
         y, kc, vc = pl.pallas_call(
             functools.partial(layer_kernel, n),
             out_shape=(jax.ShapeDtypeStruct(x_blk.shape, BF16),
@@ -343,6 +360,8 @@
                 pltpu.VMEM((q_width + ff, d), BF16),
                 pltpu.VMEM((q_width + 2 * head, seq), BF16),
                 pltpu.VMEM((seq, head), BF16),
+                pltpu.VMEM((seq, seq), F32),
+                pltpu.VMEM((seq, seq), F32),
                 pltpu.SemaphoreType.DMA((n_req,)),
                 pltpu.SemaphoreType.DMA((2, 2)),
                 pltpu.SemaphoreType.DMA((n_req, tiles)),

time: 115 us -> 108 us (0.939)
  Pallas kernels: 107 us -> 99.7 us
    pallas_call x1, Pallas kernels: 107 us -> 99.7 us  [per_device(): pl.pallas_call(functools.partial(layer_kernel, n), out_shape=(jax.ShapeDt...]
where the time goes in v2:
time: 108 us; the launch traced here: 107 us
  Pallas kernels  99.7 us (92%)
  local copies, waits for them, and re-layouts  6.49 us (6%)
    pallas_call x1, Pallas kernels, per_device(): pl.pallas_call(functools.partial(layer_kernel, n), out_shape=(jax.ShapeDt...  99.7 us
    unnamed x7, local copies, waits for them, and re-layouts  5.22 us

profile of v2, /device:TPU:97, one launch (start us, length us, event | category | flops | bytes accessed | tf_op | source)
XLA Modules:
  0.0 106.9 jit_solution(16092236751253445564)
XLA Ops:
  0.6 1.3 %reshape.9.gain_ref = f32[1,768]{1,0:T(1,128)} reshape(f32[768]{0:T(1024)} %param.7) | data formatting | bytes 6144 | tf_op jit(solution)/shard_map/reshape | solution.py:375
  1.9 99.7 %shard_map.85 = (bf16[4,512,768]{2,1,0:T(8,128)(2,1)}, bf16[4,64,512]{2,1,0:T(8,128)(2,1)}, bf16[4,64,512]{2,1,0:T(8,128)(2,1)}) custom-call(bf16[4,512,768]{2,1,0:T(8,128)(2,1)} %x_hbm.1, f32[1,768]{1,0:T(1,128)} %reshape.9.gain_ref, bf16[220,768]{1,0:T(8,128)(2,1)} %bitcast.3, bf16[120,768]{1,0:T(8,128)(2,1)} %wo_hbm.1, f32[32,512]{1,0:T(8,128)} %constant.4.clone.cos_ref, ...), custom_call_target="tpu_custom_call" | custom-call | tf_op jit(solution)/shard_map/pallas_call | solution.py:344
  101.6 0.0 copy-start.1
  101.7 0.0 copy-start
  101.7 3.8 %copy.12 = bf16[4,512,768]{2,1,0:T(8,128)(2,1)} copy(bf16[4,512,768]{2,1,0:T(8,128)(2,1)} %get-tuple-element.12) | data formatting | bytes 6291456
  105.5 0.0 copy-done.1
  105.5 0.7 copy.13
  106.2 0.0 copy-done
  106.2 0.7 copy.14
Async XLA Ops:
  101.6 3.8 %copy-start.1 = (bf16[4,64,512]{2,1,0:T(8,128)(2,1)S(1)}, bf16[4,64,512]{2,1,0:T(8,128)(2,1)}, u32[]{:S(2)}) copy-start(bf16[4,64,512]{2,1,0:T(8,128)(2,1)} %get-tuple-element.7) | copy-start | bytes 786436
  101.7 4.5 %copy-start = (bf16[4,64,512]{2,1,0:T(8,128)(2,1)S(1)}, bf16[4,64,512]{2,1,0:T(8,128)(2,1)}, u32[]{:S(2)}) copy-start(bf16[4,64,512]{2,1,0:T(8,128)(2,1)} %get-tuple-element.8) | copy-start | bytes 786436

commit v3 on v2

--- a/solution.py
+++ b/solution.py
@@ -55,10 +55,11 @@
 
 def layer_kernel(n, x_hbm, gain_ref, wi_hbm, wo_hbm, cos_ref, sin_ref, y_hbm, kc_ref, vc_ref,
                  x_v, h_v, mixed, gi, go, wq, wg, wu, wo, qkv, kt, s_a, s_b,
-                 x_sem, own_sem, y_sem, send_sem, recv_sem, psend_sem, precv_sem):
+                 x_sem, own_sem, y_sem, send_sem, recv_sem, psend_sem, precv_sem, qsend_sem, qrecv_sem):
     n_req, seq, d = x_v.shape
-    in_rows, half = gi.shape[2], gi.shape[3]
-    out_rows = go.shape[2]
+    parts, _, in_rows, lanes = gi.shape
+    out_rows, half = go.shape[2], go.shape[3]
+    mid = parts // 2
     n_dev = gi.shape[1]
     head = kc_ref.shape[1]
     q_width = wq.shape[0] - 2 * head
@@ -88,10 +89,10 @@
     me = dp * n + tp
 
     own = []
+    for p in range(parts):
+        own.append(pltpu.make_async_copy(wi_hbm.at[:, pl.ds(p * lanes, lanes)], gi.at[p, me], own_sem.at[p]))
     for h in range(2):
-        own.append(pltpu.make_async_copy(wi_hbm.at[:, pl.ds(h * half, half)], gi.at[h, me], own_sem.at[0, h]))
-    for h in range(2):
-        own.append(pltpu.make_async_copy(wo_hbm.at[:, pl.ds(h * half, half)], go.at[h, me], own_sem.at[1, h]))
+        own.append(pltpu.make_async_copy(wo_hbm.at[:, pl.ds(h * half, half)], go.at[h, me], own_sem.at[parts + h]))
     for copy in own:
         copy.start()
     x_in = [pltpu.make_async_copy(x_hbm.at[r], x_v.at[r], x_sem.at[r]) for r in range(n_req)]
@@ -105,14 +106,17 @@
     for copy in own:
         copy.wait()
 
+    def piece(rnd, h, idx):
+        return gi.at[pl.ds(h * mid, mid), idx] if rnd == 0 else go.at[h, idx]
+
     def first_ring(rnd):
         return Ring(n, a, device(a + 1, b), device(a - 1, b),
-                    lambda z, h: bufs[rnd].at[h, shard(z, b, core)],
+                    lambda z, h: piece(rnd, h, shard(z, b, core)),
                     lambda k: send_sem.at[rnd, 0, k], lambda k: recv_sem.at[rnd, 0, k])
 
     def second_ring(rnd, s):
         return Ring(n, b, device(a, b + 1), device(a, b - 1),
-                    lambda z, h: bufs[rnd].at[h, shard(s, z, core)],
+                    lambda z, h: piece(rnd, h, shard(s, z, core)),
                     lambda k: send_sem.at[rnd, 1 + s, k], lambda k: recv_sem.at[rnd, 1 + s, k])
 
     def pair_copy(rnd, s, k, mine):
@@ -125,51 +129,164 @@
             src_ref=ref, dst_ref=ref, send_sem=psend_sem.at[rnd, s, k], recv_sem=precv_sem.at[rnd, s, k],
             device_id=partner, device_id_type=MESH)
 
-    firsts = [first_ring(r) for r in range(2)]
-    seconds = [[second_ring(r, s) for s in range(n)] for r in range(2)]
+    last = first_ring(1)
 
     def finish_second(rnd, s):
-        seconds[rnd][s].finish()
+        second_ring(rnd, s).finish()
         for k in range(1, n):
             pair_copy(rnd, s, k, True).start()
 
     def start_second(rnd, s):
-        seconds[rnd][s].start()
+        second_ring(rnd, s).start()
         pair_copy(rnd, s, 0, True).start()
 
     def from_partner(rnd, s):
         for k in range(n):
             pair_copy(rnd, s, k, False).wait_recv()
 
-    firsts[0].start()
-
-    gain = gain_ref[...]
+    RIGHT, LEFT = 0, 1
+    to_right, to_left = range(mid), range(mid, parts)
+
+    def piece_copy(stage, way, p, back, arriving=False):
+        step = back + (1 if arriving else 0)
+        pos = b if stage else a
+        z = lax.rem(pos + n - step, n) if way == RIGHT else lax.rem(pos + step, n)
+        ref = gi.at[p, shard(0, z, core) if stage else shard(z, b, core)]
+        sem = p if back == 0 else parts + (p if way == RIGHT else p - mid)
+        sign = 1 if way == RIGHT else -1
+        return pltpu.make_async_remote_copy(
+            src_ref=ref, dst_ref=ref, send_sem=qsend_sem.at[stage, way, sem], recv_sem=qrecv_sem.at[stage, way, sem],
+            device_id=device(a, b + sign) if stage else device(a + sign, b), device_id_type=MESH)
+
+    def send(stage, way, p, back=0):
+        piece_copy(stage, way, p, back).start()
+
+    def arrive(stage, way, p, back=0):
+        piece_copy(stage, way, p, back, True).wait_recv()
+
+    def own_all(way):
+        for p in (*to_right, *to_left) if way == RIGHT else (*to_left, *to_right):
+            send(0, way, p)
+
+    def forward_all(way):
+        for p in to_right if way == RIGHT else to_left:
+            arrive(0, way, p)
+            send(0, way, p, 1)
+
+    def pass_on(way, p):
+        arrive(1, way, p)
+        send(1, way, p, 1)
+
+    def first_step(role, i):
+        mixed_order = tuple(p for pair in zip(to_right, to_left) for p in pair)
+        order = {1: (*to_right, *to_left), n - 1: (*to_left, *to_right)}.get(role, mixed_order)
+        p = order[i]
+        if role == 1:
+            arrive(0, RIGHT, p)
+            if p in to_right:
+                send(0, RIGHT, p, 1)
+        elif role == n - 1:
+            arrive(0, LEFT, p)
+            if p in to_left:
+                send(0, LEFT, p, 1)
+        elif role:
+            arrive(0, RIGHT if p in to_right else LEFT, p, 1)
+        send(1, RIGHT, p)
+        send(1, LEFT, p)
+        if role == 1 and i == mid - 1:
+            own_all(RIGHT)
+        if role == n - 1 and i == mid - 1:
+            own_all(LEFT)
+        if i >= mid:
+            if role == 1:
+                pass_on(RIGHT, i - mid)
+            elif role == n - 1:
+                pass_on(LEFT, i)
+            elif i == mid:
+                pass_on(RIGHT, 0)
+                pass_on(LEFT, mid)
+            elif i == parts - 1:
+                for j in range(1, mid):
+                    pass_on(RIGHT, j)
+                    pass_on(LEFT, mid + j)
+
+    def on_role(role, fn):
+        pl.when(a == role)(fn)
+
+    on_role(0, lambda: (own_all(RIGHT), own_all(LEFT)) and None)
+    on_role(1, lambda: own_all(LEFT))
+    on_role(n - 1, lambda: own_all(RIGHT))
+    on_role(2, lambda: (own_all(RIGHT), own_all(LEFT)) and None)
+
+    gain = gain_ref[...].reshape(1, d)
     ln_rows = 128
-
-    def norm_rows(r):
+    per_req = seq // ln_rows
+
+    def norm_rows(first, count):
         def body(i, carry):
-            rows = pl.ds(pl.multiple_of(i * ln_rows, ln_rows), ln_rows)
+            j = first + i
+            r = j // per_req
+            rows = pl.ds(pl.multiple_of((j - r * per_req) * ln_rows, ln_rows), ln_rows)
             xw = x_v[r, rows, :].astype(F32)
             cen = xw - jnp.mean(xw, axis=-1, keepdims=True)
             var = jnp.mean(cen * cen, axis=-1, keepdims=True)
             h_v[r, rows, :] = (cen * lax.rsqrt(var + LN_EPS) * gain).astype(BF16)
             return carry
-        lax.fori_loop(0, seq // ln_rows, body, 0)
-
-    x_in[0].wait()
-    norm_rows(0)
-    firsts[0].forward()
-    x_in[1].wait()
-    norm_rows(1)
-    firsts[0].finish()
-    start_second(0, 0)
-    for r in range(2, n_req):
-        x_in[r].wait()
-        norm_rows(r)
-    seconds[0][0].forward()
-    for s in range(1, n):
-        start_second(0, s)
-    finish_second(0, 0)
+        lax.fori_loop(0, count, body, 0)
+
+    for copy in x_in:
+        copy.wait()
+    blocks = n_req * per_req
+    share = blocks // (parts + 2)
+    norm_rows(0, blocks - share * parts)
+    for i in range(parts):
+        for role in range(n):
+            on_role(role, functools.partial(first_step, role, i))
+        norm_rows(blocks - share * (parts - i), share)
+    pair_copy(0, 0, 0, True).start()
+    on_role(1, lambda: [pass_on(LEFT, p) for p in to_left] and None)
+    on_role(n - 1, lambda: [pass_on(RIGHT, p) for p in to_right] and None)
+    for p in to_left:
+        arrive(1, RIGHT, p)
+    pair_copy(0, 0, n - 1, True).start()
+    for p in to_right:
+        arrive(1, LEFT, p)
+    pair_copy(0, 0, 1, True).start()
+    for p in to_right:
+        arrive(1, RIGHT, p, 1)
+    for p in to_left:
+        arrive(1, LEFT, p, 1)
+    pair_copy(0, 0, 2, True).start()
+
+    pl.when(a != 1)(lambda: forward_all(RIGHT))
+    pl.when(a != n - 1)(lambda: forward_all(LEFT))
+
+    @pl.when(a != 1)
+    def _():
+        for p in to_left:
+            arrive(0, RIGHT, p)
+
+    @pl.when(a != n - 1)
+    def _():
+        for p in to_right:
+            arrive(0, LEFT, p)
+
+    def later(k, fn):
+        s = lax.rem(a + k, n)
+        pl.when(s != 0)(lambda: fn(0, s))
+
+    def far_arrivals(rnd, s):
+        for p in to_right:
+            arrive(0, RIGHT, p, 1)
+        for p in to_left:
+            arrive(0, LEFT, p, 1)
+        start_second(rnd, s)
+
+    def forward_second(rnd, s):
+        second_ring(rnd, s).forward()
+
+    for k in (0, 1, 3):
+        later(k, start_second)
     from_partner(0, 0)
 
     def assemble(dst, src, rows_per, start, count):
@@ -177,8 +294,9 @@
         while row < start + count:
             blk, r0 = row // rows_per, row % rows_per
             take = min(rows_per - r0, start + count - row)
-            for h in range(2):
-                dst[row - start:row - start + take, h * half:(h + 1) * half] = src[h, blk, r0:r0 + take, :]
+            width = src.shape[3]
+            for h in range(src.shape[0]):
+                dst[row - start:row - start + take, h * width:(h + 1) * width] = src[h, blk, r0:r0 + take, :]
             row += take
 
     assemble(wq, gi, in_rows, 0, q_width + 2 * head)
@@ -227,7 +345,7 @@
             outs.append(out * jnp.concatenate(inv, axis=1))
         return jnp.concatenate(outs, axis=1)
 
-    def attend(r):
+    def attend(r, between, after):
         qkv[...] = nt_dot(wq[...], h_v[r]).astype(BF16)
         k_rot = rotate(qkv[q_width:q_width + head, :])
         kc_ref[r] = k_rot
@@ -244,23 +362,24 @@
             mixed[r, :, pl.ds(row, 2 * head)] = jnp.concatenate([out_a, out_b], axis=0).T.astype(BF16)
             return carry
 
-        lax.fori_loop(0, q_width // (2 * head), body, 0)
-
-    attend(0)
-    seconds[0][1].forward()
-    firsts[1].start()
-    attend(1)
-    finish_second(0, 1)
-    seconds[0][2].forward()
-    seconds[0][3].forward()
-    attend(2)
-    finish_second(0, 2)
-    finish_second(0, 3)
-    firsts[1].forward()
-    attend(3)
-    firsts[1].finish()
-    for s in range(n):
-        start_second(1, s)
+        pairs = q_width // (2 * head)
+        lax.fori_loop(0, pairs // 2, body, 0)
+        between()
+        lax.fori_loop(pairs // 2, pairs, body, 0)
+        after()
+
+    def slot(*todo):
+        def run():
+            for k, fn in todo:
+                later(k, fn)
+        return run
+
+    attend(0, slot(), slot((0, forward_second), (2, far_arrivals)))
+    attend(1, slot((1, forward_second)), slot((0, finish_second)))
+    attend(2, slot((3, forward_second), (1, finish_second)), slot((2, forward_second)))
+    last.start()
+    attend(3, slot((3, finish_second)), slot((2, finish_second)))
+    last.forward()
     for s in range(1, n):
         from_partner(0, s)
 
@@ -285,10 +404,21 @@
 
     for c in range(ff // chunk):
         mlp_chunk(c)
-        if c < n:
-            seconds[1][c].forward()
-        if 1 <= c <= n:
-            finish_second(1, c - 1)
+        if c == 0:
+            last.finish()
+            for s in range(n):
+                start_second(1, s)
+        if c == 1:
+            forward_second(1, 0)
+            forward_second(1, 1)
+        if c == 2:
+            forward_second(1, 2)
+            forward_second(1, 3)
+            finish_second(1, 0)
+            finish_second(1, 1)
+        if c == 3:
+            finish_second(1, 2)
+            finish_second(1, 3)
     for s in range(n):
         from_partner(1, s)
 
@@ -311,10 +441,17 @@
     for r in range(n_req):
         for t in range(tiles):
             y_copy(r, t).wait()
+    for stage in range(2):
+        for way in (RIGHT, LEFT):
+            for p in range(parts):
+                piece_copy(stage, way, p, 0).wait_send()
+            for p in to_right if way == RIGHT else to_left:
+                piece_copy(stage, way, p, 1).wait_send()
+    last.drain()
     for rnd in range(2):
-        firsts[rnd].drain()
         for s in range(n):
-            seconds[rnd][s].drain()
+            if rnd or s:
+                second_ring(rnd, s).drain()
             for k in range(n):
                 pair_copy(rnd, s, k, True).wait_send()
 
@@ -337,6 +474,7 @@
         q_width = out_rows * n_dev - ff
         head = (in_rows * n_dev - q_width - 2 * ff) // 2
         chunk = min(512, ff)
+        parts = d // 128
         cos, sin = rope_tables(seq, head)
         vmem = pl.BlockSpec(memory_space=pltpu.VMEM)
         anyw = pl.BlockSpec(memory_space=pl.ANY)
@@ -352,7 +490,7 @@
                 pltpu.VMEM((n_req, seq, d), BF16),
                 pltpu.VMEM((n_req, seq, d), BF16),
                 pltpu.VMEM((n_req, seq, q_width + ff), BF16),
-                pltpu.VMEM((2, n_dev, in_rows, d // 2), BF16),
+                pltpu.VMEM((parts, n_dev, in_rows, d // parts), BF16),
                 pltpu.VMEM((2, n_dev, out_rows, d // 2), BF16),
                 pltpu.VMEM((q_width + 2 * head, d), BF16),
                 pltpu.VMEM((chunk, d), BF16),
@@ -363,16 +501,18 @@
                 pltpu.VMEM((seq, seq), F32),
                 pltpu.VMEM((seq, seq), F32),
                 pltpu.SemaphoreType.DMA((n_req,)),
-                pltpu.SemaphoreType.DMA((2, 2)),
+                pltpu.SemaphoreType.DMA((parts + 2,)),
                 pltpu.SemaphoreType.DMA((n_req, tiles)),
                 pltpu.SemaphoreType.DMA((2, 1 + n, 6)),
                 pltpu.SemaphoreType.DMA((2, 1 + n, 6)),
                 pltpu.SemaphoreType.DMA((2, n, n)),
                 pltpu.SemaphoreType.DMA((2, n, n)),
+                pltpu.SemaphoreType.DMA((2, 2, parts + parts // 2)),
+                pltpu.SemaphoreType.DMA((2, 2, parts + parts // 2)),
             ],
             compiler_params=pltpu.CompilerParams(
                 collective_id=0, has_side_effects=True, vmem_limit_bytes=63 * 1024 * 1024),
-        )(x_blk, ln_gain.reshape(1, d), w_in_blk.T, w_out_blk, cos, sin)
+        )(x_blk, ln_gain, w_in_blk.T, w_out_blk, cos, sin)
         return y, kc.swapaxes(1, 2), vc.swapaxes(1, 2)
 
     return jax.shard_map(per_device, mesh=mesh,

time: 108 us -> 107 us (level)
  Pallas kernels: 99.7 us -> 101 us
  local copies, waits for them, and re-layouts: 6.49 us -> 5.22 us
    reshape x1 -> x0, local copies, waits for them, and re-layouts: 1.27 us -> none  [per_device(): ln_gain.reshape(1, d)]
    pallas_call x1, Pallas kernels: 99.7 us -> 101 us  [per_device(): pl.pallas_call(functools.partial(layer_kernel, n), out_shape=(jax.ShapeDt...]
where the time goes in v3:
time: 107 us
  Pallas kernels  101 us (94%)
  local copies, waits for them, and re-layouts  5.22 us (5%)
    pallas_call x1, Pallas kernels, per_device(): pl.pallas_call(functools.partial(layer_kernel, n), out_shape=(jax.ShapeDt...  101 us
    unnamed x7, local copies, waits for them, and re-layouts  5.22 us

profile of v3, /device:TPU:97, one launch (start us, length us, event | category | flops | bytes accessed | tf_op | source)
XLA Modules:
  0.0 106.8 jit_solution(7475356679446965141)
XLA Ops:
  0.6 100.9 %shard_map.85 = (bf16[4,512,768]{2,1,0:T(8,128)(2,1)}, bf16[4,64,512]{2,1,0:T(8,128)(2,1)}, bf16[4,64,512]{2,1,0:T(8,128)(2,1)}) custom-call(bf16[4,512,768]{2,1,0:T(8,128)(2,1)} %x_hbm.1, f32[768]{0:T(1024)} %gain_ref.1, bf16[220,768]{1,0:T(8,128)(2,1)} %bitcast.3, bf16[120,768]{1,0:T(8,128)(2,1)} %wo_hbm.1, f32[32,512]{1,0:T(8,128)} %constant.4.clone.cos_ref, ...), custom_call_target="tpu_custom_call" | custom-call | tf_op jit(solution)/shard_map/pallas_call | solution.py:482
  101.5 0.0 copy-start.1
  101.5 0.0 copy-start
  101.6 3.8 %copy.12 = bf16[4,512,768]{2,1,0:T(8,128)(2,1)} copy(bf16[4,512,768]{2,1,0:T(8,128)(2,1)} %get-tuple-element.12) | data formatting | bytes 6291456
  105.4 0.0 copy-done.1
  105.4 0.7 copy.13
  106.1 0.0 copy-done
  106.1 0.7 copy.14
Async XLA Ops:
  101.5 3.8 %copy-start.1 = (bf16[4,64,512]{2,1,0:T(8,128)(2,1)S(1)}, bf16[4,64,512]{2,1,0:T(8,128)(2,1)}, u32[]{:S(2)}) copy-start(bf16[4,64,512]{2,1,0:T(8,128)(2,1)} %get-tuple-element.7) | copy-start | bytes 786436
  101.5 4.5 %copy-start = (bf16[4,64,512]{2,1,0:T(8,128)(2,1)S(1)}, bf16[4,64,512]{2,1,0:T(8,128)(2,1)}, u32[]{:S(2)}) copy-start(bf16[4,64,512]{2,1,0:T(8,128)(2,1)} %get-tuple-element.8) | copy-start | bytes 786436

commit v4 on v3

--- a/solution.py
+++ b/solution.py
@@ -271,22 +271,18 @@
         for p in to_right:
             arrive(0, LEFT, p)
 
-    def later(k, fn):
-        s = lax.rem(a + k, n)
-        pl.when(s != 0)(lambda: fn(0, s))
-
-    def far_arrivals(rnd, s):
+    def far_arrivals():
         for p in to_right:
             arrive(0, RIGHT, p, 1)
         for p in to_left:
             arrive(0, LEFT, p, 1)
-        start_second(rnd, s)
 
     def forward_second(rnd, s):
         second_ring(rnd, s).forward()
 
-    for k in (0, 1, 3):
-        later(k, start_second)
+    step_a = 1 + a // (n - 1)
+    step_b = 3 - step_a
+    start_second(0, step_a)
     from_partner(0, 0)
 
     def assemble(dst, src, rows_per, start, count):
@@ -368,20 +364,26 @@
         lax.fori_loop(pairs // 2, pairs, body, 0)
         after()
 
-    def slot(*todo):
-        def run():
-            for k, fn in todo:
-                later(k, fn)
-        return run
-
-    attend(0, slot(), slot((0, forward_second), (2, far_arrivals)))
-    attend(1, slot((1, forward_second)), slot((0, finish_second)))
-    attend(2, slot((3, forward_second), (1, finish_second)), slot((2, forward_second)))
-    last.start()
-    attend(3, slot((3, finish_second)), slot((2, finish_second)))
+    def attend_0_mid():
+        pl.when(a != 2)(far_arrivals)
+        start_second(0, step_b)
+
+    def attend_1_mid():
+        forward_second(0, step_b)
+        start_second(0, 3)
+
+    def attend_2_end():
+        finish_second(0, step_b)
+        forward_second(0, 3)
+
+    nothing = lambda: None
+    attend(0, attend_0_mid, lambda: forward_second(0, step_a))
+    attend(1, attend_1_mid, nothing)
+    attend(2, lambda: finish_second(0, step_a), attend_2_end)
+    attend(3, last.start, lambda: finish_second(0, 3))
     last.forward()
-    for s in range(1, n):
-        from_partner(0, s)
+    from_partner(0, 1)
+    from_partner(0, 2)
 
     gate_at = q_width + 2 * head
     tok = 512
@@ -405,6 +407,7 @@
     for c in range(ff // chunk):
         mlp_chunk(c)
         if c == 0:
+            from_partner(0, 3)
             last.finish()
             for s in range(n):
                 start_second(1, s)

time: 107 us -> 105 us (0.981)
  Pallas kernels: 101 us -> 98.6 us
    pallas_call x1, Pallas kernels: 101 us -> 98.6 us  [per_device(): pl.pallas_call(functools.partial(layer_kernel, n), out_shape=(jax.ShapeDt...]
where the time goes in v4:
time: 105 us
  Pallas kernels  98.6 us (94%)
  local copies, waits for them, and re-layouts  5.22 us (5%)
    pallas_call x1, Pallas kernels, per_device(): pl.pallas_call(functools.partial(layer_kernel, n), out_shape=(jax.ShapeDt...  98.6 us
    unnamed x7, local copies, waits for them, and re-layouts  5.22 us

profile of v4, /device:TPU:97, one launch (start us, length us, event | category | flops | bytes accessed | tf_op | source)
XLA Modules:
  0.0 104.5 jit_solution(17985977080168349273)
XLA Ops:
  0.6 98.6 %shard_map.85 = (bf16[4,512,768]{2,1,0:T(8,128)(2,1)}, bf16[4,64,512]{2,1,0:T(8,128)(2,1)}, bf16[4,64,512]{2,1,0:T(8,128)(2,1)}) custom-call(bf16[4,512,768]{2,1,0:T(8,128)(2,1)} %x_hbm.1, f32[768]{0:T(1024)} %gain_ref.1, bf16[220,768]{1,0:T(8,128)(2,1)} %bitcast.3, bf16[120,768]{1,0:T(8,128)(2,1)} %wo_hbm.1, f32[32,512]{1,0:T(8,128)} %constant.4.clone.cos_ref, ...), custom_call_target="tpu_custom_call" | custom-call | tf_op jit(solution)/shard_map/pallas_call | solution.py:485
  99.3 0.0 copy-start.1
  99.3 0.0 copy-start
  99.3 3.8 %copy.12 = bf16[4,512,768]{2,1,0:T(8,128)(2,1)} copy(bf16[4,512,768]{2,1,0:T(8,128)(2,1)} %get-tuple-element.12) | data formatting | bytes 6291456
  103.1 0.0 copy-done.1
  103.1 0.7 copy.13
  103.8 0.0 copy-done
  103.8 0.7 copy.14
Async XLA Ops:
  99.3 3.8 %copy-start.1 = (bf16[4,64,512]{2,1,0:T(8,128)(2,1)S(1)}, bf16[4,64,512]{2,1,0:T(8,128)(2,1)}, u32[]{:S(2)}) copy-start(bf16[4,64,512]{2,1,0:T(8,128)(2,1)} %get-tuple-element.7) | copy-start | bytes 786436
  99.3 4.5 %copy-start = (bf16[4,64,512]{2,1,0:T(8,128)(2,1)S(1)}, bf16[4,64,512]{2,1,0:T(8,128)(2,1)}, u32[]{:S(2)}) copy-start(bf16[4,64,512]{2,1,0:T(8,128)(2,1)} %get-tuple-element.8) | copy-start | bytes 786436
